TPU v7x, 512 devices: a whole 4x8x8 slice. The times are simulated.
512 devices in a mesh: dp: 32 (over y, x), seq: 16 (over z, core).
Axes of the slice: x: 4, y: 8, z: 8, core: 2. Of those that a mesh axis runs over, the one named last changes fastest.
Arguments:
- states: bfloat16 [65536, 1280], P(('dp', 'seq')), parts along dimension 0, may hold values from -90 to 90
- token_kind: int32 [65536], P(('dp', 'seq')), parts along dimension 0, may hold values from 0 to 3
- episode: int32 [65536], P(('dp', 'seq')), parts along dimension 0, may hold values from 0 to 3, never falling along the last dimension, each value on 1 to 1536 neighbouring positions
- kind_table: bfloat16 [4, 1280], replicated, may hold values from -3 to 3
- w_qkv: bfloat16 [1280, 3072], replicated, may hold values from -0.15625 to 0.15625
- w_out: bfloat16 [1024, 1280], replicated, may hold values from -0.1875 to 0.1875
Outputs:
- attended: bfloat16 [65536, 1280], P(('dp', 'seq')), parts along dimension 0
There are 32 independent parts, one for each index of `dp`. A program takes and returns all parts, laid end to end along the dimension named above; an argument that names none is the same for every part. Nothing has to cross between parts.
All inputs are finite; a program needn't handle non-finite values.
Results may differ from a plain program's by a relative error of at most 0.0055.
The roundings to bfloat16 on the way count: a program that leaves them out, or rounds other values in their place, can miss the bound.
Values may be sent and summed in bfloat16 or wider, within the bound.
A program may use at most 128 MiB of HBM per device.

v0:
```python
import math

import jax
import jax.numpy as jnp
from jax import lax
from jax.sharding import PartitionSpec as P

HEADS = 16


def in_one_piece(arrays, axis, dim, along):
    both = jnp.concatenate(arrays, axis=along)
    result, at, gathered = (lax.all_gather(both, axis, axis=dim, tiled=True), 0, [])
    for a in arrays:
        gathered.append(lax.slice_in_dim(result, at, at + a.shape[along], axis=along))
        at += a.shape[along]
    return tuple(gathered)


def absorb(
    running, queries, query_place, query_episode, key_rows, value_rows, key_place, key_episode
):
    maxima, totals, summed = running
    temper = 1.0 / math.sqrt(queries.shape[2])
    scores = (
        jnp.einsum("qhd,khd->hqk", queries, key_rows, preferred_element_type=jnp.float32) * temper
    )
    allowed = (key_place[None, :] <= query_place[:, None]) & (
        key_episode[None, :] == query_episode[:, None]
    )
    scores = jnp.where(allowed[None], scores, -1e30)
    raised = jnp.maximum(maxima, jnp.max(scores, axis=2))
    shrink = jnp.exp(maxima - raised)
    weights = jnp.where(allowed[None], jnp.exp(scores - raised[:, :, None]), 0.0)
    totals = totals * shrink + jnp.sum(weights, axis=2)
    summed = summed * shrink.T[:, :, None] + jnp.einsum(
        "hqk,khd->qhd", weights.astype(jnp.bfloat16), value_rows, preferred_element_type=jnp.float32
    )
    return (raised, totals, summed)


def sweep_keys(
    running, queries, query_place, query_episode, key_rows, value_rows, key_place, key_episode
):
    length = key_rows.shape[0]
    stride = math.gcd(length, 512)

    def visit(number, current):
        offset = number * stride
        keys_here = lax.dynamic_slice_in_dim(key_rows, offset, stride, 0)
        values_here = lax.dynamic_slice_in_dim(value_rows, offset, stride, 0)
        place_here = lax.dynamic_slice_in_dim(key_place, offset, stride, 0)
        episode_here = lax.dynamic_slice_in_dim(key_episode, offset, stride, 0)
        skipped = (place_here[0] > query_place[-1]) | (episode_here[-1] < query_episode[0])
        return lax.cond(
            skipped,
            lambda s: s,
            lambda s: absorb(
                s,
                queries,
                query_place,
                query_episode,
                keys_here,
                values_here,
                place_here,
                episode_here,
            ),
            current,
        )

    return lax.fori_loop(0, length // stride, visit, running)


def fresh_state(count, heads, head_size):
    return (
        jnp.full((heads, count), -1e30, jnp.float32),
        jnp.zeros((heads, count), jnp.float32),
        jnp.zeros((count, heads, head_size), jnp.float32),
    )


def local(states, token_kind, episode, kind_table, w_qkv, w_out):
    rows = states.shape[0]
    kinds = kind_table.shape[0]
    picked = (token_kind[:, None] == jnp.arange(kinds, dtype=jnp.int32)[None, :]).astype(
        jnp.float32
    )
    added = jnp.dot(picked, kind_table.astype(jnp.float32))
    inputs = (states.astype(jnp.float32) + added).astype(jnp.bfloat16)
    projected = jnp.dot(inputs, w_qkv, preferred_element_type=jnp.float32).astype(jnp.bfloat16)
    inner = w_out.shape[0]
    head_size = inner // HEADS
    queries = projected[:, :inner].reshape(rows, HEADS, head_size)
    key_flat = projected[:, inner : 2 * inner]
    value_flat = projected[:, 2 * inner :]
    own_place = lax.axis_index("seq") * rows + jnp.arange(rows, dtype=jnp.int32)
    key_piece, value_piece, episode_piece = (
        *in_one_piece((key_flat, value_flat), "seq", 0, 1),
        lax.all_gather(episode, "seq", axis=0, tiled=True),
    )
    count = key_piece.shape[0]
    piece_place = jnp.arange(count, dtype=jnp.int32)
    maxima, totals, summed = sweep_keys(
        fresh_state(rows, HEADS, head_size),
        queries,
        own_place,
        episode,
        key_piece.reshape(count, HEADS, head_size),
        value_piece.reshape(count, HEADS, head_size),
        piece_place,
        episode_piece,
    )
    heads_out = (summed / totals.T[:, :, None]).astype(jnp.bfloat16).reshape(rows, inner)
    return jnp.dot(heads_out, w_out, preferred_element_type=jnp.float32).astype(jnp.bfloat16)


def solution(mesh):
    placed = (P(("dp", "seq"), None), P(("dp", "seq")), P(("dp", "seq")), P(), P(), P())
    return jax.shard_map(
        local, mesh=mesh, in_specs=placed, out_specs=P(("dp", "seq"), None), check_vma=False
    )
```

profile of v0, /device:TPU:391, one launch (start us, length us, event | category | flops | bytes accessed | tf_op | source)
XLA Modules:
  0.0 137.8 jit_solution(9066481034130938527)
XLA Ops:
  6.5 0.0 copy-start
  6.5 0.0 copy-start.1
  6.5 0.0 all-gather.3.cloned.1.call-start
  6.5 4.9 %convolution_convert_fusion = bf16[128,3072]{1,0:T(8,128)(2,1)S(1)} fusion(bf16[1280,3072]{1,0:T(8,128)(2,1)} %param.14, bf16[4,1280]{1,0:T(4,128)(2,1)} %param.13, bf16[128,1280]{1,0:T(8,128)(2,1)} %param.10, s32[128]{0:T(128)} %param.11), kind=kOutput, calls=%fused_computation.21 | convolution fusion | flops 1008828928 | bytes 8989184 | tf_op jit(solution)/shard_map/dot_general | solution.py:90
  11.4 0.9 concatenate.4
  12.3 0.0 all-gather.3.cloned.1.call-update
  12.3 0.7 slice.44
  13.1 1.1 copy.17
  14.2 0.0 copy-done.1
  14.2 14.9 %all-gather = s32[16,1,128]{2,1,0:T(1,128)S(1)} all-gather(s32[1,1,128]{2,1,0:T(1,128)S(1)} %bitcast.45), channel_id=1, replica_groups=mesh['dp'=32,'seq'=16] {'seq'}, dimensions={0}, use_global_device_ids=true | all-gather | bytes 8704 | tf_op jit(solution)/shard_map/all_gather | solution.py:99
  29.1 40.6 %all-gather.3.cloned.1.call-done = bf16[2048,2048]{1,0:T(8,128)(2,1)} async-done(((bf16[128,2048]{1,0:T(8,128)(2,1)}), bf16[2048,2048]{1,0:T(8,128)(2,1)}) %all-gather.3.cloned.1.call-update) | async-done | bytes 8388624 | tf_op jit(solution)/shard_map/all_gather | solution.py:13
  69.7 5.9 %fusion.25 = (bf16[2048,1024]{1,0:T(8,128)(2,1)}, bf16[2048,1024]{1,0:T(8,128)(2,1)}) fusion(bf16[2048,2048]{1,0:T(8,128)(2,1)} %all-gather.3.cloned.1.call-done), kind=kLoop, calls=%fused_computation.30 | loop fusion | bytes 16777216 | tf_op jit(solution)/shard_map/slice | solution.py:15
  75.6 6.5 %copy.16 = bf16[2048,1024]{0,1:T(8,128)(2,1)} copy(bf16[2048,1024]{1,0:T(8,128)(2,1)} %get-tuple-element.331) | data formatting | bytes 8388608 | tf_op jit(solution)/shard_map/slice | solution.py:15
  82.2 6.5 %copy.18 = bf16[2048,1024]{0,1:T(8,128)(2,1)} copy(bf16[2048,1024]{1,0:T(8,128)(2,1)} %get-tuple-element.330) | data formatting | bytes 8388608 | tf_op jit(solution)/shard_map/slice | solution.py:15
  88.7 40.9 %while.17 = (s32[]{:T(128)}, f32[16,128]{1,0:T(8,128)S(1)}, f32[16,128]{1,0:T(8,128)S(1)}, f32[128,16,64]{0,2,1:T(8,128)S(1)}, s32[2048]{0:T(1024)S(1)}, /*index...) while((s32[]{:T(128)}, f32[16,128]{1,0:T(8,128)S(1)}, ...), condition=%wide.region_5.6_spmd, body=%wide.region_0.5_spmd.sunk | while | flops 282531840 | bytes 16398717 | solution.py:71
  88.8 0.1 dynamic_slice.46
  88.8 0.1 dynamic_slice.47
  88.9 0.6 slice.51
  89.5 0.6 slice.52
  91.4 0.6 slice.53
  92.7 6.2 %conditional.2 = (f32[16,128]{1,0:T(8,128)S(1)}, f32[16,128]{1,0:T(8,128)S(1)}, f32[128,16,64]{0,2,1:T(8,128)S(1)}) conditional(s32[]{:T(128)} %bitcast.38, (s32[512]{0:T(512)S(1)}, s32[128]{0:T(128)S(1)}, s32[512]{0:T(512)S(1)}, s32[128]{0:T(128)S(1)}, bf16[2048,16,64]{0,2,1:T(8,128)(2,1)}, /*index=5*/s32[]{:T(128)}, ...), branch_computations={%region_1.3_spmd, %region_4.4_spmd} | conditional | flops 282531840 | bytes 16373784 | solution.py:55
  92.8 0.2 compare_and_fusion
  93.0 2.2 %fusion = (f32[16,128]{1,0:T(8,128)S(1)}, f32[16,512,128]{2,1,0:T(8,128)S(1)}) fusion(pred[128,512]{0,1:T(8,128)(4,1)S(1)} %compare_and_fusion, bf16[128,16,64]{0,2,1:T(8,128)(2,1)S(1)} %get-tuple-element.270, bf16[2048,16,64]{0,2,1:T(8,128)(2,1)} %get-tuple-element.268, s32[]{:T(128)} %get-tuple-element.269), kind=kOutput, calls=%fused_computation.2 | convolution fusion | flops 137361408 | bytes 5579264 | tf_op jit(solution)/shard_map/while/body/eval_jaxpr/cond/branch_0_fun/qhd,khd->hqk/dot_general | solution.py:26
  95.2 2.7 %fusion.9 = f32[128,16,64]{0,2,1:T(8,128)S(1)} fusion(f32[16,512,128]{2,1,0:T(8,128)S(1)} %get-tuple-element.329, f32[16,128]{1,0:T(8,128)S(1)} %get-tuple-element.405, pred[128,512]{0,1:T(8,128)(4,1)S(1)} %compare_and_fusion, bf16[2048,16,64]{0,2,1:T(8,128)(2,1)} %get-tuple-element.273, s32[]{:T(128)} %get-tuple-element.269, ...), kind=kOutput, calls=%fused_computation.8 | convolution fusion | flops 139722752 | bytes 6373888 | tf_op jit(solution)/shard_map/while/body/eval_jaxpr/cond/branch_0_fun/hqk,khd->qhd/dot_general | solution.py:36
  97.9 1.0 fusion.2
  99.0 0.1 dynamic_slice.46
  99.1 0.1 dynamic_slice.47
  99.1 0.6 slice.51
  99.7 0.6 slice.52
  101.6 0.6 slice.53
  103.0 6.2 %conditional.2 = (f32[16,128]{1,0:T(8,128)S(1)}, f32[16,128]{1,0:T(8,128)S(1)}, f32[128,16,64]{0,2,1:T(8,128)S(1)}) conditional(s32[]{:T(128)} %bitcast.38, (s32[512]{0:T(512)S(1)}, s32[128]{0:T(128)S(1)}, s32[512]{0:T(512)S(1)}, s32[128]{0:T(128)S(1)}, bf16[2048,16,64]{0,2,1:T(8,128)(2,1)}, /*index=5*/s32[]{:T(128)}, ...), branch_computations={%region_1.3_spmd, %region_4.4_spmd} | conditional | flops 282531840 | bytes 16373784 | solution.py:55
  103.0 0.2 compare_and_fusion
  103.2 2.2 %fusion = (f32[16,128]{1,0:T(8,128)S(1)}, f32[16,512,128]{2,1,0:T(8,128)S(1)}) fusion(pred[128,512]{0,1:T(8,128)(4,1)S(1)} %compare_and_fusion, bf16[128,16,64]{0,2,1:T(8,128)(2,1)S(1)} %get-tuple-element.270, bf16[2048,16,64]{0,2,1:T(8,128)(2,1)} %get-tuple-element.268, s32[]{:T(128)} %get-tuple-element.269), kind=kOutput, calls=%fused_computation.2 | convolution fusion | flops 137361408 | bytes 5579264 | tf_op jit(solution)/shard_map/while/body/eval_jaxpr/cond/branch_0_fun/qhd,khd->hqk/dot_general | solution.py:26
  105.4 2.7 %fusion.9 = f32[128,16,64]{0,2,1:T(8,128)S(1)} fusion(f32[16,512,128]{2,1,0:T(8,128)S(1)} %get-tuple-element.329, f32[16,128]{1,0:T(8,128)S(1)} %get-tuple-element.405, pred[128,512]{0,1:T(8,128)(4,1)S(1)} %compare_and_fusion, bf16[2048,16,64]{0,2,1:T(8,128)(2,1)} %get-tuple-element.273, s32[]{:T(128)} %get-tuple-element.269, ...), kind=kOutput, calls=%fused_computation.8 | convolution fusion | flops 139722752 | bytes 6373888 | tf_op jit(solution)/shard_map/while/body/eval_jaxpr/cond/branch_0_fun/hqk,khd->qhd/dot_general | solution.py:36
  108.1 1.0 fusion.2
  109.2 0.1 dynamic_slice.46
  109.3 0.1 dynamic_slice.47
  109.4 0.6 slice.51
  109.9 0.6 slice.52
  111.9 0.6 slice.53
  113.2 6.2 %conditional.2 = (f32[16,128]{1,0:T(8,128)S(1)}, f32[16,128]{1,0:T(8,128)S(1)}, f32[128,16,64]{0,2,1:T(8,128)S(1)}) conditional(s32[]{:T(128)} %bitcast.38, (s32[512]{0:T(512)S(1)}, s32[128]{0:T(128)S(1)}, s32[512]{0:T(512)S(1)}, s32[128]{0:T(128)S(1)}, bf16[2048,16,64]{0,2,1:T(8,128)(2,1)}, /*index=5*/s32[]{:T(128)}, ...), branch_computations={%region_1.3_spmd, %region_4.4_spmd} | conditional | flops 282531840 | bytes 16373784 | solution.py:55
  113.2 0.2 compare_and_fusion
  113.4 2.2 %fusion = (f32[16,128]{1,0:T(8,128)S(1)}, f32[16,512,128]{2,1,0:T(8,128)S(1)}) fusion(pred[128,512]{0,1:T(8,128)(4,1)S(1)} %compare_and_fusion, bf16[128,16,64]{0,2,1:T(8,128)(2,1)S(1)} %get-tuple-element.270, bf16[2048,16,64]{0,2,1:T(8,128)(2,1)} %get-tuple-element.268, s32[]{:T(128)} %get-tuple-element.269), kind=kOutput, calls=%fused_computation.2 | convolution fusion | flops 137361408 | bytes 5579264 | tf_op jit(solution)/shard_map/while/body/eval_jaxpr/cond/branch_0_fun/qhd,khd->hqk/dot_general | solution.py:26
  115.7 2.7 %fusion.9 = f32[128,16,64]{0,2,1:T(8,128)S(1)} fusion(f32[16,512,128]{2,1,0:T(8,128)S(1)} %get-tuple-element.329, f32[16,128]{1,0:T(8,128)S(1)} %get-tuple-element.405, pred[128,512]{0,1:T(8,128)(4,1)S(1)} %compare_and_fusion, bf16[2048,16,64]{0,2,1:T(8,128)(2,1)} %get-tuple-element.273, s32[]{:T(128)} %get-tuple-element.269, ...), kind=kOutput, calls=%fused_computation.8 | convolution fusion | flops 139722752 | bytes 6373888 | tf_op jit(solution)/shard_map/while/body/eval_jaxpr/cond/branch_0_fun/hqk,khd->qhd/dot_general | solution.py:36
  118.3 1.0 fusion.2
  119.4 0.1 dynamic_slice.46
  119.5 0.1 dynamic_slice.47
  119.6 0.6 slice.51
  120.1 0.6 slice.52
  122.1 0.6 slice.53
  123.4 6.2 %conditional.2 = (f32[16,128]{1,0:T(8,128)S(1)}, f32[16,128]{1,0:T(8,128)S(1)}, f32[128,16,64]{0,2,1:T(8,128)S(1)}) conditional(s32[]{:T(128)} %bitcast.38, (s32[512]{0:T(512)S(1)}, s32[128]{0:T(128)S(1)}, s32[512]{0:T(512)S(1)}, s32[128]{0:T(128)S(1)}, bf16[2048,16,64]{0,2,1:T(8,128)(2,1)}, /*index=5*/s32[]{:T(128)}, ...), branch_computations={%region_1.3_spmd, %region_4.4_spmd} | conditional | flops 282531840 | bytes 16373784 | solution.py:55
  123.4 0.2 compare_and_fusion
  123.6 2.2 %fusion = (f32[16,128]{1,0:T(8,128)S(1)}, f32[16,512,128]{2,1,0:T(8,128)S(1)}) fusion(pred[128,512]{0,1:T(8,128)(4,1)S(1)} %compare_and_fusion, bf16[128,16,64]{0,2,1:T(8,128)(2,1)S(1)} %get-tuple-element.270, bf16[2048,16,64]{0,2,1:T(8,128)(2,1)} %get-tuple-element.268, s32[]{:T(128)} %get-tuple-element.269), kind=kOutput, calls=%fused_computation.2 | convolution fusion | flops 137361408 | bytes 5579264 | tf_op jit(solution)/shard_map/while/body/eval_jaxpr/cond/branch_0_fun/qhd,khd->hqk/dot_general | solution.py:26
  125.9 2.7 %fusion.9 = f32[128,16,64]{0,2,1:T(8,128)S(1)} fusion(f32[16,512,128]{2,1,0:T(8,128)S(1)} %get-tuple-element.329, f32[16,128]{1,0:T(8,128)S(1)} %get-tuple-element.405, pred[128,512]{0,1:T(8,128)(4,1)S(1)} %compare_and_fusion, bf16[2048,16,64]{0,2,1:T(8,128)(2,1)} %get-tuple-element.273, s32[]{:T(128)} %get-tuple-element.269, ...), kind=kOutput, calls=%fused_computation.8 | convolution fusion | flops 139722752 | bytes 6373888 | tf_op jit(solution)/shard_map/while/body/eval_jaxpr/cond/branch_0_fun/hqk,khd->qhd/dot_general | solution.py:36
  128.6 1.0 fusion.2
  129.6 0.1 divide_convert_fusion
  129.7 0.0 copy-done
  129.7 1.3 convolution_convert_fusion.1
  (17 shorter events, 0.1 us)
Async XLA Ops:
  6.5 123.2 %copy-start = (bf16[1024,1280]{1,0:T(8,128)(2,1)S(1)}, bf16[1024,1280]{1,0:T(8,128)(2,1)}, u32[]{:S(2)}) copy-start(bf16[1024,1280]{1,0:T(8,128)(2,1)} %param.15) | copy-start | bytes 7864324
  6.5 7.6 %copy-start.1 = (s32[128]{0:T(128)S(1)}, s32[128]{0:T(128)}, u32[]{:S(2)}) copy-start(s32[128]{0:T(128)} %param.12) | copy-start | bytes 1540
  6.5 63.2 %all-gather.3.cloned.1.call-start = ((), (), s32[]{:S(2)}) async-start(), calls=%async_computation | async-start | bytes 8912896 | tf_op jit(solution)/shard_map/all_gather | solution.py:13
Sparse Core Ops, SparseCore 0:
  12.5 57.2 all-gather.2
where the time goes:
time: 139 us; the launch traced here: 138 us
  waiting for transfers between devices  40.6 us (29%)
  local copies, waits for them, and re-layouts  29.7 us (21%)
  matrix products  25.8 us (19%)
  blocking collectives  14.9 us (11%)
  between operations  13.5 us (10%)
  loops' own time  8.33 us (6%)
  other arithmetic  4.96 us (4%)
    all_gather x1, waiting for transfers between devices, in_one_piece(): lax.all_gather(both, axis, axis=dim, tiled=True)  40.6 us
    slice x3, local copies, waits for them, and re-layouts, in_one_piece(): lax.slice_in_dim(result, at, at + a.shape[along], axis=along)  18.9 us
    all_gather x1, blocking collectives, local(): lax.all_gather(episode, 'seq', axis=0, tiled=True)  14.9 us
    dot_general x4, matrix products, absorb(): jnp.einsum('hqk,khd->qhd', weights.astype(jnp.bfloat16), value_rows, pref...  10.7 us
    dot_general x4, matrix products, absorb(): jnp.einsum('qhd,khd->hqk', queries, key_rows, preferred_element_type=jnp....  8.94 us
    another operation x1, loops' own time, sweep_keys(): return lax.fori_loop(0, length // stride, visit, running)  8.14 us
    dot_general x1, matrix products, local(): jnp.dot(inputs, w_qkv, preferred_element_type=jnp.float32)  4.89 us
    reduce_sum x4, other arithmetic, absorb(): totals = totals * shrink + jnp.sum(weights, axis=2)  4.01 us
  transfers between devices with their start and end apart: 1, of which 1 were waited for; matrix products, arithmetic and copies ran while one was open for 1% of the time, Pallas kernels for 0%

commit v1 on v0

v1 whole, which is shorter than its diff:
```python
import functools

import jax
import jax.numpy as jnp
from jax import lax
from jax.experimental import pallas as pl
from jax.experimental.pallas import tpu as pltpu
from jax.sharding import PartitionSpec as P

HEADS = 16
MESH = pl.DeviceIdType.MESH
BF16 = jnp.bfloat16
F32 = jnp.float32
FAR = -1e30


def turn(k):
    return jnp.where(k % 2 == 1, (7 - k) // 2, 4 + k // 2)


def kernel(
    states_ref, kind_ref, episode_ref, table_ref, w_qkv_ref, w_out_ref, out_ref,
    x_ref, w_ref, wo_ref, kv_stage, q_stage, o_stage, kv_buf, q_buf, ep_buf, o_buf, k_aug, q_aug, s_ref,
    w_sem, wo_sem, kv_send, kv_recv, q_send, q_recv, ep_send, ep_recv, o_send, o_recv,
):
    rows, width = states_ref.shape
    inner = w_out_ref.shape[0]
    size = inner // HEADS
    pair = 2 * size
    me = lax.axis_index("seq")
    z, c = me // 2, me % 2

    barrier = pltpu.get_barrier_semaphore()

    def greet(k, _):
        pl.semaphore_signal(barrier, inc=1, device_id={"seq": (me + k) % HEADS}, device_id_type=MESH)
        return 0

    lax.fori_loop(1, HEADS, greet, 0)

    def chip(k):
        return (z + turn(k)) % 8

    def weights(k, part):
        at = pl.multiple_of(part * inner + chip(k) * pair, pair)
        return pltpu.make_async_copy(w_qkv_ref.at[:, pl.ds(at, pair)], w_ref.at[part, k], w_sem.at[part, k])

    def fetch_kv(k, _):
        weights(k, 1).start()
        weights(k, 2).start()
        return 0

    def fetch_q(k, _):
        weights(k, 0).start()
        return 0

    lax.fori_loop(0, 8, fetch_kv, 0)
    lax.fori_loop(0, 8, fetch_q, 0)
    w_out_copy = pltpu.make_async_copy(w_out_ref, wo_ref, wo_sem)
    w_out_copy.start()

    kinds = jnp.broadcast_to(kind_ref[...].astype(F32), (rows, rows)).T
    for at in range(0, width, rows):
        table = table_ref[:, at : at + rows].astype(F32)
        added = jnp.broadcast_to(table[3:4], (rows, rows))
        for kind in range(3):
            added = jnp.where(kinds == float(kind), table[kind : kind + 1], added)
        x_ref[:, at : at + rows] = (states_ref[:, at : at + rows].astype(F32) + added).astype(BF16)

    pl.semaphore_wait(barrier, HEADS - 1)

    ep_buf[me] = episode_ref[...]

    def episode_copy(k):
        return pltpu.make_async_remote_copy(
            src_ref=episode_ref, dst_ref=ep_buf.at[me], send_sem=ep_send.at[k], recv_sem=ep_recv.at[me],
            device_id={"seq": (me + k) % HEADS}, device_id_type=MESH,
        )

    def send_episode(k, _):
        episode_copy(k).start()
        return 0

    lax.fori_loop(1, HEADS, send_episode, 0)

    def kv_copy(k, core):
        return pltpu.make_async_remote_copy(
            src_ref=kv_stage.at[k, core], dst_ref=kv_buf.at[me], send_sem=kv_send.at[k, core], recv_sem=kv_recv.at[me],
            device_id={"seq": chip(k) * 2 + core}, device_id_type=MESH,
        )

    def q_copy(k, core):
        return pltpu.make_async_remote_copy(
            src_ref=q_stage.at[k, core], dst_ref=q_buf.at[me], send_sem=q_send.at[k, core], recv_sem=q_recv.at[me],
            device_id={"seq": chip(k) * 2 + core}, device_id_type=MESH,
        )

    def project(k, part):
        weights(k, part).wait()
        return jnp.dot(x_ref[...], w_ref[part, k], preferred_element_type=F32).astype(BF16).T

    def make_kv(k):
        keys = project(k, 1)
        values = project(k, 2)
        for core in range(2):
            kv_stage[k, core, :size] = keys[core * size : (core + 1) * size]
            kv_stage[k, core, size:] = values[core * size : (core + 1) * size]

    def make_q(k):
        queries = project(k, 0)
        for core in range(2):
            q_stage[k, core] = queries[core * size : (core + 1) * size]

    def do_kv(k, _):
        make_kv(k)
        kv_copy(k, 0).start()
        kv_copy(k, 1).start()
        return 0

    def do_q(k, _):
        make_q(k)
        q_copy(k, 0).start()
        q_copy(k, 1).start()
        return 0

    lax.fori_loop(0, 7, do_kv, 0)
    make_kv(7)
    kv_copy(7, 1 - c).start()
    kv_buf[me] = kv_stage[7, c]
    lax.fori_loop(0, 7, do_q, 0)
    make_q(7)
    q_copy(7, 1 - c).start()
    q_buf[me] = q_stage[7, c]

    def arrived(copy, j):
        @pl.when(j != me)
        def _():
            copy.wait_recv()

    def from_peer(dst, sem, j):
        return pltpu.make_async_remote_copy(
            src_ref=dst.at[j], dst_ref=dst.at[j], send_sem=sem.at[j], recv_sem=sem.at[j],
            device_id={"seq": j}, device_id_type=MESH,
        )

    lines = lax.broadcasted_iota(jnp.int32, (size, rows), 0)

    def take_kv(j, _):
        arrived(from_peer(ep_buf, ep_recv, j), j)
        arrived(from_peer(kv_buf, kv_recv, j), j)
        other = jnp.where((lines < 4) & (lines != ep_buf[j]), 1.0, 0.0).astype(BF16)
        k_aug[pl.ds(pl.multiple_of(j * rows, rows), rows)] = jnp.concatenate([kv_buf[j, :size], other], axis=0).T
        return 0

    def take_q(j, _):
        arrived(from_peer(q_buf, q_recv, j), j)
        same = jnp.where(lines == ep_buf[j], FAR, 0.0).astype(BF16)
        q_aug[j] = jnp.concatenate([q_buf[j] * 0.125, same], axis=0)
        return 0

    lax.fori_loop(0, HEADS, take_kv, 0)
    lax.fori_loop(0, HEADS, take_q, 0)

    block = 2 * rows
    later = lax.broadcasted_iota(jnp.int32, (block, block), 0) > lax.broadcasted_iota(jnp.int32, (block, block), 1)

    def o_copy(b, core):
        return pltpu.make_async_remote_copy(
            src_ref=o_stage.at[b, core], dst_ref=o_buf.at[me], send_sem=o_send.at[b, core], recv_sem=o_recv.at[me],
            device_id={"seq": 2 * b + core}, device_id_type=MESH,
        )

    for b in range(8):
        queries = jnp.concatenate([q_aug[2 * b], q_aug[2 * b + 1]], axis=1)
        top = None
        for a in range(b + 1):
            scores = jnp.dot(k_aug[a * block : (a + 1) * block], queries, preferred_element_type=F32)
            if a == b:
                scores = jnp.where(later, FAR, scores)
            s_ref[a * block : (a + 1) * block] = scores
            here = jnp.max(scores.reshape(block // 8, 8, block), axis=0)
            top = here if top is None else jnp.maximum(top, here)
        top = jnp.max(top, axis=0, keepdims=True)
        total, summed = None, None
        for a in range(b + 1):
            weight = jnp.exp(s_ref[a * block : (a + 1) * block] - top)
            part = jnp.sum(weight.reshape(block // 8, 8, block), axis=0)
            values = jnp.concatenate([kv_buf[2 * a, size:], kv_buf[2 * a + 1, size:]], axis=1)
            mixed = jnp.dot(values, weight.astype(BF16), preferred_element_type=F32)
            total = part if total is None else total + part
            summed = mixed if summed is None else summed + mixed
        total = jnp.sum(total, axis=0, keepdims=True)
        result = (summed / total).astype(BF16)
        for core in range(2):
            o_stage[b, core] = result[:, core * rows : (core + 1) * rows]

            @pl.when(2 * b + core != me)
            def _():
                o_copy(b, core).start()

            @pl.when(2 * b + core == me)
            def _():
                o_buf[me] = o_stage[b, core]

    def take_o(j, _):
        arrived(from_peer(o_buf, o_recv, j), j)
        return 0

    lax.fori_loop(0, HEADS, take_o, 0)
    w_out_copy.wait()
    heads_out = o_buf[...].reshape(inner, rows).T
    out_ref[...] = jnp.dot(heads_out, wo_ref[...], preferred_element_type=F32).astype(BF16)

    def sent(k, _):
        kv_copy(k, 0).wait_send()
        kv_copy(k, 1).wait_send()
        q_copy(k, 0).wait_send()
        q_copy(k, 1).wait_send()
        return 0

    def episode_sent(k, _):
        episode_copy(k).wait_send()
        return 0

    def o_sent(b, _):
        for core in range(2):
            @pl.when(2 * b + core != me)
            def _():
                o_copy(b, core).wait_send()
        return 0

    lax.fori_loop(1, HEADS, episode_sent, 0)
    lax.fori_loop(0, 7, sent, 0)
    kv_copy(7, 1 - c).wait_send()
    q_copy(7, 1 - c).wait_send()
    lax.fori_loop(0, 8, o_sent, 0)


def local(states, token_kind, episode, kind_table, w_qkv, w_out):
    rows, width = states.shape
    inner = w_out.shape[0]
    size = inner // HEADS
    vmem = pl.BlockSpec(memory_space=pltpu.VMEM)
    hbm = pl.BlockSpec(memory_space=pl.ANY)
    dma = pltpu.SemaphoreType.DMA
    return pl.pallas_call(
        kernel,
        name="episode_attention",
        out_shape=jax.ShapeDtypeStruct((rows, width), BF16),
        in_specs=[vmem, vmem, vmem, vmem, hbm, hbm],
        out_specs=vmem,
        scratch_shapes=[
            pltpu.VMEM((rows, width), BF16),
            pltpu.VMEM((3, 8, width, 2 * size), BF16),
            pltpu.VMEM((inner, width), BF16),
            pltpu.VMEM((8, 2, 2 * size, rows), BF16),
            pltpu.VMEM((8, 2, size, rows), BF16),
            pltpu.VMEM((8, 2, size, rows), BF16),
            pltpu.VMEM((HEADS, 2 * size, rows), BF16),
            pltpu.VMEM((HEADS, size, rows), BF16),
            pltpu.VMEM((HEADS, 1, rows), jnp.int32),
            pltpu.VMEM((HEADS, size, rows), BF16),
            pltpu.VMEM((HEADS * rows, 2 * size), BF16),
            pltpu.VMEM((HEADS, 2 * size, rows), BF16),
            pltpu.VMEM((HEADS * rows, 2 * rows), F32),
            dma((3, 8)), dma(()),
            dma((8, 2)), dma((HEADS,)),
            dma((8, 2)), dma((HEADS,)),
            dma((HEADS,)), dma((HEADS,)),
            dma((8, 2)), dma((HEADS,)),
        ],
        compiler_params=pltpu.CompilerParams(
            collective_id=0, has_side_effects=True, vmem_limit_bytes=48 * 1024 * 1024
        ),
    )(states, token_kind.reshape(1, rows), episode.reshape(1, rows), kind_table, w_qkv, w_out)


def solution(mesh):
    placed = (P(("dp", "seq"), None), P(("dp", "seq")), P(("dp", "seq")), P(), P(), P())
    return jax.shard_map(
        local, mesh=mesh, in_specs=placed, out_specs=P(("dp", "seq"), None), check_vma=False
    )
```

time: 139 us -> 48.3 us (0.35)
  the two profiles are of different devices: /device:TPU:391 before, /device:TPU:1 now
where the time goes in v1:
time: 48.3 us; the launch traced here: 48 us
  Pallas kernels  42.6 us (88%)
  local copies, waits for them, and re-layouts  5.45 us (11%)
    pallas_call x1, Pallas kernels, local(): pl.pallas_call(kernel, name='episode_attention', out_shape=jax.ShapeDtype...  42.6 us
    unnamed x11, local copies, waits for them, and re-layouts  5.45 us

profile of v1, /device:TPU:1, one launch (start us, length us, event | category | flops | bytes accessed | tf_op | source)
XLA Modules:
  0.0 48.0 jit_solution(8588174059394415949)
XLA Ops:
  0.0 0.0 copy-start
  0.0 1.7 %copy-done = bf16[1024,1280]{1,0:T(8,128)(2,1)S(1)} copy-done((bf16[1024,1280]{1,0:T(8,128)(2,1)S(1)}, bf16[1024,1280]{1,0:T(8,128)(2,1)}, u32[]{:S(2)}) %copy-start) | copy-done | bytes 2621464
  1.7 0.0 copy-start.1
  1.7 1.0 %copy-done.1 = bf16[128,1280]{1,0:T(8,128)(2,1)S(1)} copy-done((bf16[128,1280]{1,0:T(8,128)(2,1)S(1)}, bf16[128,1280]{1,0:T(8,128)(2,1)}, u32[]{:S(2)}) %copy-start.1) | copy-done | bytes 327704
  2.7 0.0 copy-start.2
  2.7 0.7 %copy-done.2 = bf16[4,1280]{1,0:T(4,128)(2,1)S(1)} copy-done((bf16[4,1280]{1,0:T(4,128)(2,1)S(1)}, bf16[4,1280]{1,0:T(4,128)(2,1)}, u32[]{:S(2)}) %copy-start.2) | copy-done | bytes 10264
  3.4 0.0 copy-start.3
  3.4 0.7 %copy-done.3 = s32[128]{0:T(128)S(1)} copy-done((s32[128]{0:T(128)S(1)}, s32[128]{0:T(128)}, u32[]{:S(2)}) %copy-start.3) | copy-done | bytes 536
  4.1 0.0 copy-start.4
  4.1 0.7 %copy-done.4 = s32[128]{0:T(128)S(1)} copy-done((s32[128]{0:T(128)S(1)}, s32[128]{0:T(128)}, u32[]{:S(2)}) %copy-start.4) | copy-done | bytes 536
  4.7 42.6 %episode_attention.1 = bf16[128,1280]{1,0:T(8,128)(2,1)S(1)} custom-call(bf16[128,1280]{1,0:T(8,128)(2,1)S(1)} %copy-done.1, s32[1,128]{1,0:T(1,128)S(1)} %bitcast.2, s32[1,128]{1,0:T(1,128)S(1)} %bitcast.3, bf16[4,1280]{1,0:T(4,128)(2,1)S(1)} %copy-done.2, bf16[1280,3072]{1,0:T(8,128)(2,1)} %w_qkv_ref.1, bf16[1024,1280]{1,0:T(8,128)(2,1)S(1)} %copy-done), custom_call_target="tpu_custom_call" | custom-call | tf_op jit(solution)/shard_map/episode_attention/pallas_call | solution.py:246
  47.3 0.7 %copy.8 = bf16[128,1280]{1,0:T(8,128)(2,1)} copy(bf16[128,1280]{1,0:T(8,128)(2,1)S(1)} %episode_attention.1) | data formatting | bytes 655360
Async XLA Ops:
  0.0 1.7 %copy-start = (bf16[1024,1280]{1,0:T(8,128)(2,1)S(1)}, bf16[1024,1280]{1,0:T(8,128)(2,1)}, u32[]{:S(2)}) copy-start(bf16[1024,1280]{1,0:T(8,128)(2,1)} %w_out_ref.1) | copy-start | bytes 7864324
  1.7 1.0 %copy-start.1 = (bf16[128,1280]{1,0:T(8,128)(2,1)S(1)}, bf16[128,1280]{1,0:T(8,128)(2,1)}, u32[]{:S(2)}) copy-start(bf16[128,1280]{1,0:T(8,128)(2,1)} %states_ref.1) | copy-start | bytes 983044
  2.7 0.7 %copy-start.2 = (bf16[4,1280]{1,0:T(4,128)(2,1)S(1)}, bf16[4,1280]{1,0:T(4,128)(2,1)}, u32[]{:S(2)}) copy-start(bf16[4,1280]{1,0:T(4,128)(2,1)} %table_ref.1) | copy-start | bytes 30724
  3.4 0.7 %copy-start.3 = (s32[128]{0:T(128)S(1)}, s32[128]{0:T(128)}, u32[]{:S(2)}) copy-start(s32[128]{0:T(128)} %param.7) | copy-start | bytes 1540
  4.1 0.7 %copy-start.4 = (s32[128]{0:T(128)S(1)}, s32[128]{0:T(128)}, u32[]{:S(2)}) copy-start(s32[128]{0:T(128)} %param.8) | copy-start | bytes 1540

commit v2 on v1

v2 whole, which is shorter than its diff:
```python
import jax
import jax.numpy as jnp
from jax import lax
from jax.experimental import pallas as pl
from jax.experimental.pallas import tpu as pltpu
from jax.sharding import PartitionSpec as P

HEADS = 16
CHIPS = 8
MESH = pl.DeviceIdType.MESH
BF16 = jnp.bfloat16
F32 = jnp.float32
FAR = -1e30
AHEAD = 4


def turn(k):
    return jnp.where(k % 2 == 1, (7 - k) // 2, 4 + k // 2)


def kernel(
    states_hbm, kind_hbm, episode_hbm, table_hbm, w_qkv_hbm, w_out_hbm, out_ref,
    states_ref, kind_ref, table_ref, x_ref, w_ref, wo_ref, kv_stage, q_stage, o_stage, kv_buf, q_buf, ep_buf, o_buf,
    k_aug, s_ref, p_ref, v_ref, h_ref, acc_ref,
    in_sem, w_sem, kv_send, kv_recv, q_send, q_recv, ep_send, ep_recv, o_send, o_recv,
):
    rows, width = states_ref.shape
    inner = wo_ref.shape[0]
    size = inner // HEADS
    pair = 2 * size
    block = 2 * rows
    me = lax.axis_index("seq")
    z, c = me // 2, me % 2

    barrier = pltpu.get_barrier_semaphore()

    def greet(k, _):
        pl.semaphore_signal(barrier, inc=1, device_id={"seq": (me + k) % HEADS}, device_id_type=MESH)
        return 0

    lax.fori_loop(1, HEADS, greet, 0)

    loads = [
        pltpu.make_async_copy(states_hbm, states_ref, in_sem.at[0]),
        pltpu.make_async_copy(kind_hbm, kind_ref, in_sem.at[1]),
        pltpu.make_async_copy(table_hbm, table_ref, in_sem.at[2]),
        pltpu.make_async_copy(episode_hbm, ep_buf.at[me], in_sem.at[3]),
    ]

    def w_out_copy(slot):
        g = to_chip((slot + 7) % CHIPS)
        return pltpu.make_async_copy(
            w_out_hbm.at[pl.ds(pl.multiple_of(g * pair, pair), pair)],
            wo_ref.at[pl.ds(pl.multiple_of(slot * pair, pair), pair)], in_sem.at[4],
        )

    for load in loads:
        load.start()

    def to_chip(k):
        return (z + turn(k)) % CHIPS

    def from_chip(k):
        return (z + CHIPS - turn(k)) % CHIPS

    def weights(k, part):
        at = pl.multiple_of(part * inner + to_chip(k) * pair, pair)
        return pltpu.make_async_copy(
            w_qkv_hbm.at[:, pl.ds(at, pair)], w_ref.at[part, k], w_sem.at[0 if part == 0 else 1, k]
        )

    def landed(ref, sem):
        pltpu.make_async_copy(ref, ref, sem).wait()

    def fetch_kv(k, _):
        weights(k, 1).start()
        weights(k, 2).start()
        return 0

    lax.fori_loop(0, AHEAD, fetch_kv, 0)

    for load in loads:
        load.wait()
    kinds = jnp.broadcast_to(kind_ref[...].astype(F32), (rows, rows)).T
    for at in range(0, width, rows):
        table = table_ref[:, at : at + rows].astype(F32)
        added = jnp.broadcast_to(table[3:4], (rows, rows))
        for kind in range(3):
            added = jnp.where(kinds == float(kind), table[kind : kind + 1], added)
        x_ref[:, at : at + rows] = (states_ref[:, at : at + rows].astype(F32) + added).astype(BF16)

    def episode_copy(k):
        return pltpu.make_async_remote_copy(
            src_ref=ep_buf.at[me], dst_ref=ep_buf.at[me], send_sem=ep_send, recv_sem=ep_recv,
            device_id={"seq": (me + k) % HEADS}, device_id_type=MESH,
        )

    def kv_copy(k, core, lane=0):
        return pltpu.make_async_remote_copy(
            src_ref=kv_stage.at[k, core], dst_ref=kv_buf.at[me], send_sem=kv_send.at[lane], recv_sem=kv_recv.at[z],
            device_id={"seq": to_chip(k) * 2 + core}, device_id_type=MESH,
        )

    def q_copy(k, core, lane=0):
        return pltpu.make_async_remote_copy(
            src_ref=q_stage.at[k, core], dst_ref=q_buf.at[me], send_sem=q_send.at[lane], recv_sem=q_recv.at[z],
            device_id={"seq": to_chip(k) * 2 + core}, device_id_type=MESH,
        )

    def o_copy(b, core, lane=0):
        return pltpu.make_async_remote_copy(
            src_ref=o_stage.at[b, core], dst_ref=o_buf.at[me], send_sem=o_send.at[lane], recv_sem=o_recv.at[z],
            device_id={"seq": 2 * b + core}, device_id_type=MESH,
        )

    def project(k, part):
        return jnp.dot(x_ref[...], w_ref[part, k], preferred_element_type=F32).astype(BF16).T

    def make_kv(k):
        landed(w_ref.at[pl.ds(1, 2), k], w_sem.at[1, k])
        keys = project(k, 1)
        values = project(k, 2)
        for core in range(2):
            kv_stage[k, core, :size] = keys[core * size : (core + 1) * size]
            kv_stage[k, core, size:] = values[core * size : (core + 1) * size]

    def make_q(k):
        landed(w_ref.at[0, k], w_sem.at[0, k])
        queries = project(k, 0)
        for core in range(2):
            q_stage[k, core] = queries[core * size : (core + 1) * size]

    def fetch_later(k):
        @pl.when(k < CHIPS)
        def _():
            weights(k, 1).start()
            weights(k, 2).start()

        @pl.when((k >= CHIPS) & (k < 2 * CHIPS))
        def _():
            weights(k - CHIPS, 0).start()

    def send_kv(k, _):
        kv_copy(k, 0).start()
        kv_copy(k, 1).start()
        return 0

    def send_q(k, _):
        q_copy(k, 0).start()
        q_copy(k, 1).start()
        return 0

    def stage_kv(k, _):
        fetch_later(k + AHEAD)
        make_kv(k)
        return 0

    def stage_q(k, _):
        fetch_later(k + CHIPS + AHEAD)
        make_q(k)
        return 0

    def do_kv(k, _):
        stage_kv(k, 0)
        return send_kv(k, 0)

    def do_q(k, _):
        stage_q(k, 0)
        return send_q(k, 0)

    def send_episode(k, _):
        episode_copy(k).start()
        return 0

    kv_early = jnp.where(z < 4, 7, jnp.where(z < 7, 3, 1))
    q_early = jnp.where(z < 2, 7, jnp.where(z == 2, 3, 0))
    lax.fori_loop(0, kv_early, stage_kv, 0)

    @pl.when(z < 4)
    def _():
        stage_kv(7, 0)

    lax.fori_loop(0, q_early, stage_q, 0)

    pl.semaphore_wait(barrier, HEADS - 1)
    lax.fori_loop(1, HEADS, send_episode, 0)
    lax.fori_loop(0, kv_early, send_kv, 0)
    lax.fori_loop(kv_early, 7, do_kv, 0)

    @pl.when(z >= 4)
    def _():
        stage_kv(7, 0)

    kv_copy(7, 1 - c, 1).start()
    kv_buf[me] = kv_stage[7, c]
    lax.fori_loop(0, q_early, send_q, 0)
    lax.fori_loop(q_early, 7, do_q, 0)

    stage_q(7, 0)
    q_copy(7, 1 - c, 1).start()
    q_buf[me] = q_stage[7, c]

    def fetch_w_out(slot, _):
        w_out_copy(slot).start()
        return 0

    lax.fori_loop(0, CHIPS, fetch_w_out, 0)

    lines = lax.broadcasted_iota(jnp.int32, (size, rows), 0)

    def take_kv(j):
        other = jnp.where((lines < 4) & (lines != ep_buf[j]), 1.0, 0.0).astype(BF16)
        at = pl.multiple_of(j * rows, rows)
        k_aug[pl.ds(at, rows)] = jnp.concatenate([kv_buf[j, :size], other], axis=0).T
        v_ref[:, pl.ds(at, rows)] = kv_buf[j, size:]

    def take_chip(k, _):
        g = from_chip(k)
        landed(kv_buf.at[pl.ds(2 * g, 2)], kv_recv.at[g])
        take_kv(2 * g)
        take_kv(2 * g + 1)
        return 0

    partner = z * 2 + 1 - c
    landed(ep_buf.at[pl.ds(0, HEADS - 1)], ep_recv)
    take_kv(me)
    landed(kv_buf.at[partner], kv_recv.at[z])
    take_kv(partner)
    lax.fori_loop(0, 7, take_chip, 0)

    later = lax.broadcasted_iota(jnp.int32, (block, block), 0) > lax.broadcasted_iota(jnp.int32, (block, block), 1)

    def attend(b):
        queries = []
        for j in (2 * b, 2 * b + 1):
            same = jnp.where(lines == ep_buf[j], FAR, 0.0).astype(BF16)
            queries.append(jnp.concatenate([q_buf[j] * 0.125, same], axis=0))
        queries = jnp.concatenate(queries, axis=1)
        top = None
        for a in range(b + 1):
            scores = jnp.dot(k_aug[a * block : (a + 1) * block], queries, preferred_element_type=F32)
            if a == b:
                scores = jnp.where(later, FAR, scores)
            s_ref[a * block : (a + 1) * block] = scores
            here = jnp.max(scores.reshape(block // 8, 8, block), axis=0)
            top = here if top is None else jnp.maximum(top, here)
        top = jnp.max(top, axis=0, keepdims=True)
        total = None
        for a in range(b + 1):
            weight = jnp.exp(s_ref[a * block : (a + 1) * block] - top)
            here = jnp.sum(weight.reshape(block // 8, 8, block), axis=0)
            total = here if total is None else total + here
            p_ref[a * block : (a + 1) * block] = weight.astype(BF16)
        end = (b + 1) * block
        summed = jnp.dot(v_ref[:, :end], p_ref[:end], preferred_element_type=F32)
        total = jnp.sum(total, axis=0, keepdims=True)
        result = (summed / total).astype(BF16)
        for core in range(2):
            o_stage[b, core] = result[:, core * rows : (core + 1) * rows]

    def attend_any(b):
        lax.switch(b, [lambda b=b: attend(b) for b in range(CHIPS)])

    landed(q_buf.at[partner], q_recv.at[z])
    attend_any(z)
    o_copy(z, 1 - c, 1).start()
    o_buf[me] = o_stage[z, c]

    def answer(k, _):
        b = from_chip(k)
        landed(q_buf.at[pl.ds(2 * b, 2)], q_recv.at[b])
        attend_any(b)
        o_copy(b, 0).start()
        o_copy(b, 1).start()
        return 0

    lax.fori_loop(0, 7, answer, 0)

    def take_o(g, slot):
        h_ref[:, pl.ds(pl.multiple_of(slot * pair, pair), pair)] = jnp.concatenate(
            [o_buf[2 * g], o_buf[2 * g + 1]], axis=0
        ).T

    def take_chip_o(k, _):
        g = to_chip(k)
        landed(o_buf.at[pl.ds(2 * g, 2)], o_recv.at[g])
        take_o(g, k + 1)
        return 0

    landed(wo_ref, in_sem.at[4])
    landed(o_buf.at[partner], o_recv.at[z])
    take_o(z, 0)
    lax.fori_loop(0, 5, take_chip_o, 0)
    most = 6 * pair
    acc_ref[...] = jnp.dot(h_ref[:, :most], wo_ref[:most], preferred_element_type=F32)
    lax.fori_loop(5, 7, take_chip_o, 0)
    rest = jnp.dot(h_ref[:, most:], wo_ref[most:], preferred_element_type=F32)
    out_ref[...] = (acc_ref[...] + rest).astype(BF16)

    landed(ep_buf.at[pl.ds(0, HEADS - 1)], ep_send)
    landed(kv_stage.at[pl.ds(0, 7)], kv_send.at[0])
    landed(q_stage.at[pl.ds(0, 7)], q_send.at[0])
    landed(o_stage.at[pl.ds(0, 7)], o_send.at[0])
    landed(kv_stage.at[7, 0], kv_send.at[1])
    landed(q_stage.at[7, 0], q_send.at[1])
    landed(o_stage.at[7, 0], o_send.at[1])


def local(states, token_kind, episode, kind_table, w_qkv, w_out):
    rows, width = states.shape
    inner = w_out.shape[0]
    size = inner // HEADS
    hbm = pl.BlockSpec(memory_space=pltpu.HBM)
    dma = pltpu.SemaphoreType.DMA
    return pl.pallas_call(
        kernel,
        name="episode_attention",
        out_shape=jax.ShapeDtypeStruct((rows, width), BF16),
        in_specs=[hbm] * 6,
        out_specs=pl.BlockSpec(memory_space=pltpu.VMEM),
        scratch_shapes=[
            pltpu.VMEM((rows, width), BF16),
            pltpu.VMEM((1, rows), jnp.int32),
            pltpu.VMEM(kind_table.shape, BF16),
            pltpu.VMEM((rows, width), BF16),
            pltpu.VMEM((3, CHIPS, width, 2 * size), BF16),
            pltpu.VMEM((inner, width), BF16),
            pltpu.VMEM((CHIPS, 2, 2 * size, rows), BF16),
            pltpu.VMEM((CHIPS, 2, size, rows), BF16),
            pltpu.VMEM((CHIPS, 2, size, rows), BF16),
            pltpu.VMEM((HEADS, 2 * size, rows), BF16),
            pltpu.VMEM((HEADS, size, rows), BF16),
            pltpu.VMEM((HEADS, 1, rows), jnp.int32),
            pltpu.VMEM((HEADS, size, rows), BF16),
            pltpu.VMEM((HEADS * rows, 2 * size), BF16),
            pltpu.VMEM((HEADS * rows, 2 * rows), F32),
            pltpu.VMEM((HEADS * rows, 2 * rows), BF16),
            pltpu.VMEM((size, HEADS * rows), BF16),
            pltpu.VMEM((rows, inner), BF16),
            pltpu.VMEM((rows, width), F32),
            dma((5,)), dma((2, CHIPS)),
            dma((2,)), dma((CHIPS,)),
            dma((2,)), dma((CHIPS,)),
            dma(()), dma(()),
            dma((2,)), dma((CHIPS,)),
        ],
        compiler_params=pltpu.CompilerParams(
            collective_id=0, has_side_effects=True, vmem_limit_bytes=48000000
        ),
    )(*[pltpu.with_memory_space_constraint(v, pltpu.HBM) for v in (states, token_kind.reshape(1, rows), episode.reshape(1, rows), kind_table, w_qkv, w_out)])


def solution(mesh):
    placed = (P(("dp", "seq"), None), P(("dp", "seq")), P(("dp", "seq")), P(), P(), P())
    return jax.shard_map(
        local, mesh=mesh, in_specs=placed, out_specs=P(("dp", "seq"), None), check_vma=False
    )
```

time: 48.3 us -> 40.5 us (0.84)
  local copies, waits for them, and re-layouts: 5.45 us -> 0.73 us
  Pallas kernels: 42.6 us -> 39.7 us
    unnamed x11 -> x1, local copies, waits for them, and re-layouts: 5.45 us -> 0.73 us
    pallas_call x1, Pallas kernels: 42.6 us -> 39.7 us  [local(): pl.pallas_call(kernel, name='episode_attention', out_shape=jax.ShapeDtype...]
where the time goes in v2:
time: 40.5 us; the launch traced here: 40.4 us
  Pallas kernels  39.7 us (98%)
  local copies, waits for them, and re-layouts  0.73 us (2%)
    pallas_call x1, Pallas kernels, local(): pl.pallas_call(kernel, name='episode_attention', out_shape=jax.ShapeDtype...  39.7 us

profile of v2, /device:TPU:1, one launch (start us, length us, event | category | flops | bytes accessed | tf_op | source)
XLA Modules:
  0.0 40.4 jit_solution(7160275280941458614)
XLA Ops:
  0.0 39.7 %episode_attention.1 = bf16[128,1280]{1,0:T(8,128)(2,1)S(1)} custom-call(bf16[128,1280]{1,0:T(8,128)(2,1)} %states_hbm.1, s32[1,128]{1,0:T(1,128)} %bitcast.2, s32[1,128]{1,0:T(1,128)} %bitcast.3, bf16[4,1280]{1,0:T(4,128)(2,1)} %table_hbm.1, bf16[1280,3072]{1,0:T(8,128)(2,1)} %w_qkv_hbm.1, bf16[1024,1280]{1,0:T(8,128)(2,1)} %w_out_hbm.1), custom_call_target="tpu_custom_call" | custom-call | tf_op jit(solution)/shard_map/episode_attention/pallas_call | solution.py:315
  39.7 0.7 %copy.8 = bf16[128,1280]{1,0:T(8,128)(2,1)} copy(bf16[128,1280]{1,0:T(8,128)(2,1)S(1)} %episode_attention.1) | data formatting | bytes 655360

commit v3 on v2

--- a/solution.py
+++ b/solution.py
@@ -14,15 +14,23 @@
 AHEAD = 4
 
 
-def turn(k):
-    return jnp.where(k % 2 == 1, (7 - k) // 2, 4 + k // 2)
+NEAR = 4
+OWN = CHIPS - 1
+
+
+def packed(turns):
+    return sum(turn << (3 * at) for at, turn in enumerate(turns))
+
+
+KV_TURNS = packed((2, 6, 1, 7, 4, 3, 5, 0))
+Q_TURNS = packed((4, 3, 5, 2, 6, 1, 7, 0))
 
 
 def kernel(
     states_hbm, kind_hbm, episode_hbm, table_hbm, w_qkv_hbm, w_out_hbm, out_ref,
     states_ref, kind_ref, table_ref, x_ref, w_ref, wo_ref, kv_stage, q_stage, o_stage, kv_buf, q_buf, ep_buf, o_buf,
-    k_aug, s_ref, p_ref, v_ref, h_ref, acc_ref,
-    in_sem, w_sem, kv_send, kv_recv, q_send, q_recv, ep_send, ep_recv, o_send, o_recv,
+    k_aug, s_ref, v_ref, h_ref, acc_ref,
+    in_sem, w_sem, beyond, kv_send, kv_recv, q_send, q_recv, ep_send, ep_recv, o_send, o_recv,
 ):
     rows, width = states_ref.shape
     inner = wo_ref.shape[0]
@@ -35,10 +43,18 @@
     barrier = pltpu.get_barrier_semaphore()
 
     def greet(k, _):
-        pl.semaphore_signal(barrier, inc=1, device_id={"seq": (me + k) % HEADS}, device_id_type=MESH)
-        return 0
-
-    lax.fori_loop(1, HEADS, greet, 0)
+        pl.semaphore_signal(barrier, inc=1, device_id={"seq": (2 * z + k) % HEADS}, device_id_type=MESH)
+        return 0
+
+    partner = z * 2 + 1 - c
+    lax.fori_loop(2, 6, greet, 0)
+    lax.fori_loop(HEADS - 4, HEADS, greet, 0)
+    pl.semaphore_signal(barrier, inc=1, device_id={"seq": partner}, device_id_type=MESH)
+
+    def tell(side, chips):
+        pl.semaphore_signal(
+            beyond.at[side], inc=1, device_id={"seq": (z + chips) % CHIPS * 2 + c}, device_id_type=MESH
+        )
 
     loads = [
         pltpu.make_async_copy(states_hbm, states_ref, in_sem.at[0]),
@@ -48,7 +64,7 @@
     ]
 
     def w_out_copy(slot):
-        g = to_chip((slot + 7) % CHIPS)
+        g = to_chip(Q_TURNS, (slot + OWN) % CHIPS)
         return pltpu.make_async_copy(
             w_out_hbm.at[pl.ds(pl.multiple_of(g * pair, pair), pair)],
             wo_ref.at[pl.ds(pl.multiple_of(slot * pair, pair), pair)], in_sem.at[4],
@@ -57,14 +73,15 @@
     for load in loads:
         load.start()
 
-    def to_chip(k):
-        return (z + turn(k)) % CHIPS
-
-    def from_chip(k):
-        return (z + CHIPS - turn(k)) % CHIPS
+    def to_chip(turns, k):
+        return (z + ((turns >> (3 * k)) & 7)) % CHIPS
+
+    def from_chip(turns, k):
+        return (z + CHIPS - ((turns >> (3 * k)) & 7)) % CHIPS
 
     def weights(k, part):
-        at = pl.multiple_of(part * inner + to_chip(k) * pair, pair)
+        g = to_chip(KV_TURNS if part else Q_TURNS, k)
+        at = pl.multiple_of(part * inner + g * pair, pair)
         return pltpu.make_async_copy(
             w_qkv_hbm.at[:, pl.ds(at, pair)], w_ref.at[part, k], w_sem.at[0 if part == 0 else 1, k]
         )
@@ -89,22 +106,22 @@
             added = jnp.where(kinds == float(kind), table[kind : kind + 1], added)
         x_ref[:, at : at + rows] = (states_ref[:, at : at + rows].astype(F32) + added).astype(BF16)
 
-    def episode_copy(k):
+    def episode_copy(k, core):
         return pltpu.make_async_remote_copy(
             src_ref=ep_buf.at[me], dst_ref=ep_buf.at[me], send_sem=ep_send, recv_sem=ep_recv,
-            device_id={"seq": (me + k) % HEADS}, device_id_type=MESH,
+            device_id={"seq": to_chip(KV_TURNS, k) * 2 + core}, device_id_type=MESH,
         )
 
     def kv_copy(k, core, lane=0):
         return pltpu.make_async_remote_copy(
             src_ref=kv_stage.at[k, core], dst_ref=kv_buf.at[me], send_sem=kv_send.at[lane], recv_sem=kv_recv.at[z],
-            device_id={"seq": to_chip(k) * 2 + core}, device_id_type=MESH,
+            device_id={"seq": to_chip(KV_TURNS, k) * 2 + core}, device_id_type=MESH,
         )
 
     def q_copy(k, core, lane=0):
         return pltpu.make_async_remote_copy(
             src_ref=q_stage.at[k, core], dst_ref=q_buf.at[me], send_sem=q_send.at[lane], recv_sem=q_recv.at[z],
-            device_id={"seq": to_chip(k) * 2 + core}, device_id_type=MESH,
+            device_id={"seq": to_chip(Q_TURNS, k) * 2 + core}, device_id_type=MESH,
         )
 
     def o_copy(b, core, lane=0):
@@ -141,6 +158,13 @@
             weights(k - CHIPS, 0).start()
 
     def send_kv(k, _):
+        @pl.when(k == NEAR)
+        def _():
+            pl.semaphore_wait(beyond.at[0], 1)
+            pl.semaphore_wait(beyond.at[1], 1)
+
+        episode_copy(k, 0).start()
+        episode_copy(k, 1).start()
         kv_copy(k, 0).start()
         kv_copy(k, 1).start()
         return 0
@@ -168,29 +192,30 @@
         stage_q(k, 0)
         return send_q(k, 0)
 
-    def send_episode(k, _):
-        episode_copy(k).start()
-        return 0
-
-    kv_early = jnp.where(z < 4, 7, jnp.where(z < 7, 3, 1))
-    q_early = jnp.where(z < 2, 7, jnp.where(z == 2, 3, 0))
+    late = (z == 0) & (c == 0) & (lax.axis_index("dp") == 0)
+    kv_early = jnp.where(z < 3, 7, jnp.where(z == 3, 5, jnp.where(z < 6, 2, 1)))
+    kv_early = jnp.where(late, 2, kv_early)
+    q_early = jnp.where((z < 2) & jnp.logical_not(late), 7, 0)
+    own_early = (z < 3) & jnp.logical_not(late)
     lax.fori_loop(0, kv_early, stage_kv, 0)
 
-    @pl.when(z < 4)
+    @pl.when(own_early)
     def _():
         stage_kv(7, 0)
 
     lax.fori_loop(0, q_early, stage_q, 0)
 
-    pl.semaphore_wait(barrier, HEADS - 1)
-    lax.fori_loop(1, HEADS, send_episode, 0)
+    pl.semaphore_wait(barrier, 9)
+    tell(0, 2)
+    tell(1, 6)
     lax.fori_loop(0, kv_early, send_kv, 0)
     lax.fori_loop(kv_early, 7, do_kv, 0)
 
-    @pl.when(z >= 4)
+    @pl.when(jnp.logical_not(own_early))
     def _():
         stage_kv(7, 0)
 
+    episode_copy(7, 1 - c).start()
     kv_copy(7, 1 - c, 1).start()
     kv_buf[me] = kv_stage[7, c]
     lax.fori_loop(0, q_early, send_q, 0)
@@ -215,13 +240,12 @@
         v_ref[:, pl.ds(at, rows)] = kv_buf[j, size:]
 
     def take_chip(k, _):
-        g = from_chip(k)
+        g = from_chip(KV_TURNS, k)
         landed(kv_buf.at[pl.ds(2 * g, 2)], kv_recv.at[g])
         take_kv(2 * g)
         take_kv(2 * g + 1)
         return 0
 
-    partner = z * 2 + 1 - c
     landed(ep_buf.at[pl.ds(0, HEADS - 1)], ep_recv)
     take_kv(me)
     landed(kv_buf.at[partner], kv_recv.at[z])
@@ -245,14 +269,13 @@
             here = jnp.max(scores.reshape(block // 8, 8, block), axis=0)
             top = here if top is None else jnp.maximum(top, here)
         top = jnp.max(top, axis=0, keepdims=True)
-        total = None
+        total, summed = None, None
         for a in range(b + 1):
             weight = jnp.exp(s_ref[a * block : (a + 1) * block] - top)
             here = jnp.sum(weight.reshape(block // 8, 8, block), axis=0)
             total = here if total is None else total + here
-            p_ref[a * block : (a + 1) * block] = weight.astype(BF16)
-        end = (b + 1) * block
-        summed = jnp.dot(v_ref[:, :end], p_ref[:end], preferred_element_type=F32)
+            mixed = jnp.dot(v_ref[:, a * block : (a + 1) * block], weight.astype(BF16), preferred_element_type=F32)
+            summed = mixed if summed is None else summed + mixed
         total = jnp.sum(total, axis=0, keepdims=True)
         result = (summed / total).astype(BF16)
         for core in range(2):
@@ -267,7 +290,7 @@
     o_buf[me] = o_stage[z, c]
 
     def answer(k, _):
-        b = from_chip(k)
+        b = from_chip(Q_TURNS, k)
         landed(q_buf.at[pl.ds(2 * b, 2)], q_recv.at[b])
         attend_any(b)
         o_copy(b, 0).start()
@@ -282,7 +305,7 @@
         ).T
 
     def take_chip_o(k, _):
-        g = to_chip(k)
+        g = to_chip(Q_TURNS, k)
         landed(o_buf.at[pl.ds(2 * g, 2)], o_recv.at[g])
         take_o(g, k + 1)
         return 0
@@ -334,11 +357,10 @@
             pltpu.VMEM((HEADS, size, rows), BF16),
             pltpu.VMEM((HEADS * rows, 2 * size), BF16),
             pltpu.VMEM((HEADS * rows, 2 * rows), F32),
-            pltpu.VMEM((HEADS * rows, 2 * rows), BF16),
             pltpu.VMEM((size, HEADS * rows), BF16),
             pltpu.VMEM((rows, inner), BF16),
             pltpu.VMEM((rows, width), F32),
-            dma((5,)), dma((2, CHIPS)),
+            dma((5,)), dma((2, CHIPS)), pltpu.SemaphoreType.REGULAR((2,)),
             dma((2,)), dma((CHIPS,)),
             dma((2,)), dma((CHIPS,)),
             dma(()), dma(()),

time: 40.5 us -> 39.2 us (0.968)
  Pallas kernels: 39.7 us -> 38.3 us
    pallas_call x1, Pallas kernels: 39.7 us -> 38.3 us  [local(): pl.pallas_call(kernel, name='episode_attention', out_shape=jax.ShapeDtype...]
where the time goes in v3:
time: 39.2 us; the launch traced here: 39.1 us
  Pallas kernels  38.3 us (98%)
  local copies, waits for them, and re-layouts  0.73 us (2%)
    pallas_call x1, Pallas kernels, local(): pl.pallas_call(kernel, name='episode_attention', out_shape=jax.ShapeDtype...  38.3 us

profile of v3, /device:TPU:1, one launch (start us, length us, event | category | flops | bytes accessed | tf_op | source)
XLA Modules:
  0.0 39.1 jit_solution(11020122041639548774)
XLA Ops:
  0.0 38.3 %episode_attention.1 = bf16[128,1280]{1,0:T(8,128)(2,1)S(1)} custom-call(bf16[128,1280]{1,0:T(8,128)(2,1)} %states_hbm.1, s32[1,128]{1,0:T(1,128)} %bitcast.2, s32[1,128]{1,0:T(1,128)} %bitcast.3, bf16[4,1280]{1,0:T(4,128)(2,1)} %table_hbm.1, bf16[1280,3072]{1,0:T(8,128)(2,1)} %w_qkv_hbm.1, bf16[1024,1280]{1,0:T(8,128)(2,1)} %w_out_hbm.1), custom_call_target="tpu_custom_call" | custom-call | tf_op jit(solution)/shard_map/episode_attention/pallas_call | solution.py:338
  38.3 0.7 %copy.8 = bf16[128,1280]{1,0:T(8,128)(2,1)} copy(bf16[128,1280]{1,0:T(8,128)(2,1)S(1)} %episode_attention.1) | data formatting | bytes 655360

commit v4 on v3

--- a/solution.py
+++ b/solution.py
@@ -237,7 +237,7 @@
         other = jnp.where((lines < 4) & (lines != ep_buf[j]), 1.0, 0.0).astype(BF16)
         at = pl.multiple_of(j * rows, rows)
         k_aug[pl.ds(at, rows)] = jnp.concatenate([kv_buf[j, :size], other], axis=0).T
-        v_ref[:, pl.ds(at, rows)] = kv_buf[j, size:]
+        v_ref[:size, pl.ds(at, rows)] = kv_buf[j, size:]
 
     def take_chip(k, _):
         g = from_chip(KV_TURNS, k)
@@ -246,6 +246,7 @@
         take_kv(2 * g + 1)
         return 0
 
+    v_ref[size:] = jnp.ones((16, HEADS * rows), BF16)
     landed(ep_buf.at[pl.ds(0, HEADS - 1)], ep_recv)
     take_kv(me)
     landed(kv_buf.at[partner], kv_recv.at[z])
@@ -261,7 +262,7 @@
             queries.append(jnp.concatenate([q_buf[j] * 0.125, same], axis=0))
         queries = jnp.concatenate(queries, axis=1)
         top = None
-        for a in range(b + 1):
+        for a in (b, *range(b)):
             scores = jnp.dot(k_aug[a * block : (a + 1) * block], queries, preferred_element_type=F32)
             if a == b:
                 scores = jnp.where(later, FAR, scores)
@@ -269,15 +270,12 @@
             here = jnp.max(scores.reshape(block // 8, 8, block), axis=0)
             top = here if top is None else jnp.maximum(top, here)
         top = jnp.max(top, axis=0, keepdims=True)
-        total, summed = None, None
+        summed = None
         for a in range(b + 1):
             weight = jnp.exp(s_ref[a * block : (a + 1) * block] - top)
-            here = jnp.sum(weight.reshape(block // 8, 8, block), axis=0)
-            total = here if total is None else total + here
             mixed = jnp.dot(v_ref[:, a * block : (a + 1) * block], weight.astype(BF16), preferred_element_type=F32)
             summed = mixed if summed is None else summed + mixed
-        total = jnp.sum(total, axis=0, keepdims=True)
-        result = (summed / total).astype(BF16)
+        result = (summed[:size] / summed[size : size + 1]).astype(BF16)
         for core in range(2):
             o_stage[b, core] = result[:, core * rows : (core + 1) * rows]
 
@@ -357,7 +355,7 @@
             pltpu.VMEM((HEADS, size, rows), BF16),
             pltpu.VMEM((HEADS * rows, 2 * size), BF16),
             pltpu.VMEM((HEADS * rows, 2 * rows), F32),
-            pltpu.VMEM((size, HEADS * rows), BF16),
+            pltpu.VMEM((size + 16, HEADS * rows), BF16),
             pltpu.VMEM((rows, inner), BF16),
             pltpu.VMEM((rows, width), F32),
             dma((5,)), dma((2, CHIPS)), pltpu.SemaphoreType.REGULAR((2,)),

time: 39.2 us -> 39.2 us (level)
  no operation moved by 1% of the time
where the time goes in v4:
time: 39.2 us; the launch traced here: 39.1 us
  Pallas kernels  38.3 us (98%)
  local copies, waits for them, and re-layouts  0.73 us (2%)
    pallas_call x1, Pallas kernels, local(): pl.pallas_call(kernel, name='episode_attention', out_shape=jax.ShapeDtype...  38.3 us

profile of v4, /device:TPU:1, one launch (start us, length us, event | category | flops | bytes accessed | tf_op | source)
XLA Modules:
  0.0 39.1 jit_solution(14030060004883175874)
XLA Ops:
  0.0 38.3 %episode_attention.1 = bf16[128,1280]{1,0:T(8,128)(2,1)S(1)} custom-call(bf16[128,1280]{1,0:T(8,128)(2,1)} %states_hbm.1, s32[1,128]{1,0:T(1,128)} %bitcast.2, s32[1,128]{1,0:T(1,128)} %bitcast.3, bf16[4,1280]{1,0:T(4,128)(2,1)} %table_hbm.1, bf16[1280,3072]{1,0:T(8,128)(2,1)} %w_qkv_hbm.1, bf16[1024,1280]{1,0:T(8,128)(2,1)} %w_out_hbm.1), custom_call_target="tpu_custom_call" | custom-call | tf_op jit(solution)/shard_map/episode_attention/pallas_call | solution.py:336
  38.4 0.7 %copy.8 = bf16[128,1280]{1,0:T(8,128)(2,1)} copy(bf16[128,1280]{1,0:T(8,128)(2,1)S(1)} %episode_attention.1) | data formatting | bytes 655360
